TPU v7x, 32 devices: a whole 2x2x4 slice. The times are simulated.
32 devices in a mesh: texel: 8 (over y, x, core), light: 4 (over z).
Axes of the slice: x: 2, y: 2, z: 4, core: 2. Of those that a mesh axis runs over, the one named last changes fastest.
Arguments:
- tex_feat: bfloat16 [8192, 512], P('texel'), may hold values from -18 to 18
- light_feat: bfloat16 [6144, 512], P('light'), may hold values from -0.25 to 0.25
- sketch: bfloat16 [6144, 256], P('light'), may hold values from -0.078125 to 0.078125
- row_counts: int32 [8], replicated, may hold values from 1 to 1024, 4096 in all
Outputs:
- basis: float32 [8192, 256], P('texel')
- coeffs: float32 [256, 6144], P('texel', 'light')
Inputs may be any that keep to these rules, and one draw needn't show every extreme that they name: row_counts sums to 8 * 512; some entry equals 1024.
All inputs are finite; a program needn't handle non-finite values.
Results may differ from a plain program's by a relative error of at most 0.0034.
Values sent between devices are 32-bit elements; how exact they have to be, the bound alone decides.
A program may use at most 64 MiB of HBM per device.

v0:
```python
import jax
import jax.numpy as jnp
from jax import lax
from jax.sharding import PartitionSpec as P


def on_device(tex_feat, light_feat, sketch, row_counts):
    capacity = tex_feat.shape[0]
    own_count = row_counts[lax.axis_index("texel")]
    valid_total = jnp.sum(row_counts).astype(jnp.float32)
    logits = lax.dot_general(
        tex_feat, light_feat, (((1,), (1,)), ((), ())), preferred_element_type=jnp.float32
    )
    tile_block = jnp.sin(logits).astype(jnp.bfloat16)
    row_valid = (lax.iota(jnp.int32, capacity) < own_count).astype(jnp.float32)
    partial_value = (
        jnp.dot(tile_block, sketch, preferred_element_type=jnp.float32) * row_valid[:, None]
    )
    sketched = lax.psum(partial_value, "light")
    gram_local = jnp.dot(sketched.T, sketched, precision=lax.Precision.HIGHEST)
    gram_matrix = lax.psum(gram_local, "texel") / valid_total
    factor = jnp.linalg.cholesky(gram_matrix)
    basis = jax.scipy.linalg.solve_triangular(factor, sketched.T, lower=True).T
    basis_half = basis.astype(jnp.bfloat16)
    coeffs = lax.psum_scatter(
        lax.dot_general(
            basis_half, tile_block, (((0,), (0,)), ((), ())), preferred_element_type=jnp.float32
        ),
        "texel",
        scatter_dimension=0,
        tiled=True,
    ) / jnp.sqrt(valid_total)
    return (basis, coeffs)


def solution(mesh):
    placed = (P("texel", None), P("light", None), P("light", None), P())
    return jax.shard_map(
        on_device,
        mesh=mesh,
        in_specs=placed,
        out_specs=(P("texel", None), P("texel", "light")),
        check_vma=False,
    )
```

profile of v0, /device:TPU:0, one launch (start us, length us, event | category | flops | bytes accessed | tf_op | source)
XLA Modules:
  0.0 261.9 jit_solution(2642677506085759507)
XLA Ops:
  7.2 1.3 dynamic_slice.3
  8.6 0.6 fusion.10
  9.3 23.0 %sine_convert_fusion = bf16[1024,1536]{1,0:T(8,128)(2,1)S(1)} fusion(bf16[1024,512]{1,0:T(8,128)(2,1)} %param.4, bf16[1536,512]{1,0:T(8,128)(2,1)S(1)} %copy-done), kind=kOutput, calls=%fused_computation.2 | convolution fusion | flops 1612185600 | bytes 5767168 | tf_op jit(solution)/shard_map/dot_general | solution.py:11
  32.2 1.7 copy-done.2
  33.9 1.9 convolution_multiply_fusion
  35.9 54.7 %all-reduce.4.cloned.1.call-done = f32[1024,256]{1,0:T(8,128)} async-done(((f32[1024,256]{1,0:T(8,128)}), f32[1024,256]{1,0:T(8,128)}) %all-reduce.4.cloned.1.call-update) | async-done | bytes 1048592 | tf_op jit(solution)/shard_map/psum | solution.py:19
  90.6 4.1 %fusion.12 = f32[256,256]{0,1:T(8,128)} fusion(f32[1024,256]{1,0:T(8,128)} %all-reduce.4.cloned.1.call-done), kind=kOutput, calls=%fused_computation.37 | convolution fusion | flops 805306368 | bytes 1310720 | tf_op jit(solution)/shard_map/dot_general | solution.py:20
  96.3 51.8 %all-reduce.6.cloned.1.call-done = f32[256,256]{0,1:T(8,128)} async-done(((f32[256,256]{0,1:T(8,128)}), f32[256,256]{0,1:T(8,128)}) %all-reduce.6.cloned.1.call-update) | async-done | bytes 262160 | tf_op jit(solution)/shard_map/psum | solution.py:21
  148.1 1.0 broadcast_divide_fusion
  149.2 1.0 fusion.4
  150.2 11.7 %cholesky.50 = f32[128,128]{1,0:T(8,128)S(1)} custom-call(f32[128,128]{1,0:T(8,128)S(1)} %cholesky.118), custom_call_target="Cholesky" | custom-call | tf_op jit(solution)/shard_map/jit(cholesky)/cholesky | solution.py:22
  162.0 9.8 %custom-call.15 = f32[1,128,128]{1,2,0:T(8,128)S(1)} custom-call(f32[1,128,128]{2,1,0:T(8,128)S(1)} %get-tuple-element.25), custom_call_target="InvertDiagBlocksLowerTriangular" | custom-call | tf_op jit(solution)/shard_map/jit(cholesky)/cholesky | solution.py:22
  172.3 11.7 %cholesky.105 = f32[128,128]{1,0:T(8,128)S(1)} custom-call(f32[128,128]{1,0:T(8,128)S(1)} %convolution_subtract_fusion.1), custom_call_target="Cholesky" | custom-call | tf_op jit(solution)/shard_map/jit(cholesky)/cholesky | solution.py:22
  184.1 0.7 compare_reduce_fusion
  186.1 4.1 %while.1 = (s32[]{:T(128)}, f32[256,256]{1,0:T(8,128)S(1)}, s32[2,2]{1,0:T(2,128)S(1)}, f32[2,128,128]{2,1,0:T(8,128)S(1)}, s32[]{:T(128)}) while((s32[]{:T(128)}, f32[256,256]{1,0:T(8,128)S(1)}, s32[2,2]{1,0:T(2,128)S(1)}, f32[2,128,128]{2,1,0:T(8,128)S(1)}, s32[]{:T(128)}) %tuple.28), condition=%wide.while_cond, body=%wide.while_body.sunk | while | flops 2 | bytes 131189 | solution.py:23
  186.9 1.4 bitcast_dynamic-update-slice_fusion.2
  188.8 1.4 bitcast_dynamic-update-slice_fusion.2
  190.9 20.5 %custom-call.16 = f32[2,128,128]{1,2,0:T(8,128)S(1)} custom-call(f32[2,128,128]{2,1,0:T(8,128)} %copy-done.5), custom_call_target="InvertDiagBlocksLowerTriangular" | custom-call | tf_op jit(solution)/shard_map/jit(_solve_triangular)/triangular_solve | solution.py:23
  212.0 1.0 convolution_subtract_fusion
  213.7 2.2 fusion.2
  215.9 1.1 maximum_bitcast_fusion
  217.0 2.5 copy.8
  219.5 34.2 %reduce-scatter.2.cloned.1.call-done = f32[32,1536]{1,0:T(8,128)} async-done(((f32[256,1536]{1,0:T(8,128)}), f32[32,1536]{1,0:T(8,128)}) %reduce-scatter.2.cloned.1.call-update) | async-done | bytes 196624 | tf_op jit(solution)/shard_map/reduce_scatter | solution.py:25
  253.7 1.6 broadcast_divide_fusion.1
  (37 shorter events, 4.9 us)
Async XLA Ops:
  7.2 2.1 copy-start
  7.2 83.5 %all-reduce.4.cloned.1.call-start = ((), (), s32[]{:S(2)}) async-start(), calls=%async_computation.1 | async-start | bytes 2097152 | tf_op jit(solution)/shard_map/psum | solution.py:19
  9.2 24.7 %copy-start.4 = (bf16[1536,256]{1,0:T(8,128)(2,1)S(1)}, bf16[1536,256]{1,0:T(8,128)(2,1)}, u32[]{:S(2)}) copy-start(bf16[1536,256]{1,0:T(8,128)(2,1)} %param.6) | copy-start | bytes 2359300
  32.2 1.7 copy-start.2
  35.8 59.2 %copy-start.6 = (s32[8]{0:T(128)S(1)}, s32[8]{0:T(128)}, u32[]{:S(2)}) copy-start(s32[8]{0:T(128)} %param.7) | copy-start | bytes 100
  35.9 112.3 %all-reduce.6.cloned.1.call-start = ((), (), s32[]{:S(2)}) async-start(), calls=%async_computation.2 | async-start | bytes 524288 | tf_op jit(solution)/shard_map/psum | solution.py:21
  90.6 120.7 %copy-start.1 = (f32[1024,256]{1,0:T(8,128)S(1)}, f32[1024,256]{1,0:T(8,128)}, u32[]{:S(2)}) copy-start(f32[1024,256]{1,0:T(8,128)} %all-reduce.4.cloned.1.call-done) | copy-start | bytes 3145732
  94.8 158.9 %reduce-scatter.2.cloned.1.call-start = ((), (), s32[]{:S(2)}) async-start(), calls=%async_computation.3 | async-start | bytes 1769472 | tf_op jit(solution)/shard_map/reduce_scatter | solution.py:25
  190.2 0.7 copy-start.5
  211.4 2.3 copy-start.3
Sparse Core Ops, SparseCore 0:
  36.0 54.6 all-reduce.3
  94.9 53.1 all-reduce.5
  216.0 37.6 reduce-scatter.1
where the time goes:
time: 262 us
  waiting for transfers between devices  141 us (54%)
  other arithmetic  60.4 us (23%)
  matrix products  34 us (13%)
  between operations  15.8 us (6%)
  local copies, waits for them, and re-layouts  10.3 us (4%)
    psum x1, waiting for transfers between devices, on_device(): sketched = lax.psum(partial_value, 'light')  54.7 us
    psum x1, waiting for transfers between devices, on_device(): gram_matrix = lax.psum(gram_local, 'texel') / valid_total  51.8 us
    reduce_scatter x1, waiting for transfers between devices, on_device(): lax.psum_scatter(lax.dot_general(basis_half, tile_block, (((0,), (0,)), (...  34.2 us
    another operation x6, other arithmetic, on_device(): factor = jnp.linalg.cholesky(gram_matrix)  34 us
    dot_general x1, matrix products, on_device(): lax.dot_general(tex_feat, light_feat, (((1,), (1,)), ((), ())), preferred...  23 us
    another operation x3, other arithmetic, on_device(): basis = jax.scipy.linalg.solve_triangular(factor, sketched.T, lower=True).T  20.5 us
  transfers between devices with their start and end apart: 3, of which 3 were waited for; matrix products, arithmetic and copies ran while one was open for 2% of the time, Pallas kernels for 0%

commit v1 on v0

--- a/solution.py
+++ b/solution.py
@@ -16,7 +16,8 @@
     partial_value = (
         jnp.dot(tile_block, sketch, preferred_element_type=jnp.float32) * row_valid[:, None]
     )
-    sketched = lax.psum(partial_value, "light")
+    mat_out = jax.lax.all_gather(partial_value, "light")
+    sketched = jnp.sum(mat_out, 0)
     gram_local = jnp.dot(sketched.T, sketched, precision=lax.Precision.HIGHEST)
     gram_matrix = lax.psum(gram_local, "texel") / valid_total
     factor = jnp.linalg.cholesky(gram_matrix)

time: 262 us -> 292 us (1.11)
  waiting for transfers between devices: 141 us -> 169 us
    all_gather x0 -> x1, waiting for transfers between devices: none -> 83.6 us  [on_device(): mat_out = jax.lax.all_gather(partial_value, 'light')]
    psum x1 -> x0, waiting for transfers between devices: 54.7 us -> none  [on_device(): sketched = lax.psum(partial_value, 'light')]
  transfers between devices with their start and end apart: 3 -> 3, of which waited for: 3 -> 3; matrix products, arithmetic and copies ran while one was open for 2% -> 1% of each run, Pallas kernels for 0% -> 0%
where the time goes in v1:
time: 292 us; the launch traced here: 291 us
  waiting for transfers between devices  169 us (58%)
  other arithmetic  63.1 us (22%)
  matrix products  32.3 us (11%)
  between operations  15.9 us (5%)
  local copies, waits for them, and re-layouts  10.5 us (4%)
    all_gather x1, waiting for transfers between devices, on_device(): mat_out = jax.lax.all_gather(partial_value, 'light')  83.6 us
    psum x1, waiting for transfers between devices, on_device(): gram_matrix = lax.psum(gram_local, 'texel') / valid_total  50.9 us
    reduce_scatter x1, waiting for transfers between devices, on_device(): lax.psum_scatter(lax.dot_general(basis_half, tile_block, (((0,), (0,)), (...  34.3 us
    another operation x6, other arithmetic, on_device(): factor = jnp.linalg.cholesky(gram_matrix)  34 us
    dot_general x1, matrix products, on_device(): lax.dot_general(tex_feat, light_feat, (((1,), (1,)), ((), ())), preferred...  23 us
    another operation x3, other arithmetic, on_device(): basis = jax.scipy.linalg.solve_triangular(factor, sketched.T, lower=True).T  20.5 us
  transfers between devices with their start and end apart: 3, of which 3 were waited for; matrix products, arithmetic and copies ran while one was open for 1% of the time, Pallas kernels for 0%

profile of v1, /device:TPU:0, one launch (start us, length us, event | category | flops | bytes accessed | tf_op | source)
XLA Modules:
  0.0 291.3 jit_solution(13809831102737779570)
XLA Ops:
  7.2 1.3 dynamic_slice.3
  9.3 23.0 %sine_convert_fusion = bf16[1024,1536]{1,0:T(8,128)(2,1)S(1)} fusion(bf16[1024,512]{1,0:T(8,128)(2,1)} %param.4, bf16[1536,512]{1,0:T(8,128)(2,1)S(1)} %copy-done), kind=kOutput, calls=%fused_computation.2 | convolution fusion | flops 1612185600 | bytes 5767168 | tf_op jit(solution)/shard_map/dot_general | solution.py:11
  32.2 1.7 copy-done.1
  33.9 1.9 convolution_multiply_fusion
  35.9 83.6 %all-gather.3.cloned.1.call-done = f32[4096,256]{1,0:T(8,128)} async-done(((f32[1024,256]{1,0:T(8,128)}), f32[4096,256]{1,0:T(8,128)}) %all-gather.3.cloned.1.call-update) | async-done | bytes 4194320 | tf_op jit(solution)/shard_map/all_gather | solution.py:19
  119.5 2.6 reduce_sum.18
  122.1 2.5 fusion.12
  126.2 50.9 %all-reduce.3.cloned.1.call-done = f32[256,256]{0,1:T(8,128)} async-done(((f32[256,256]{0,1:T(8,128)}), f32[256,256]{0,1:T(8,128)}) %all-reduce.3.cloned.1.call-update) | async-done | bytes 262160 | tf_op jit(solution)/shard_map/psum | solution.py:22
  177.2 1.0 broadcast_divide_fusion
  178.3 1.0 fusion.4
  179.3 11.7 %cholesky.50 = f32[128,128]{1,0:T(8,128)S(1)} custom-call(f32[128,128]{1,0:T(8,128)S(1)} %cholesky.118), custom_call_target="Cholesky" | custom-call | tf_op jit(solution)/shard_map/jit(cholesky)/cholesky | solution.py:23
  191.1 9.8 %custom-call.15 = f32[1,128,128]{1,2,0:T(8,128)S(1)} custom-call(f32[1,128,128]{2,1,0:T(8,128)S(1)} %get-tuple-element.25), custom_call_target="InvertDiagBlocksLowerTriangular" | custom-call | tf_op jit(solution)/shard_map/jit(cholesky)/cholesky | solution.py:23
  201.4 11.7 %cholesky.105 = f32[128,128]{1,0:T(8,128)S(1)} custom-call(f32[128,128]{1,0:T(8,128)S(1)} %convolution_subtract_fusion.1), custom_call_target="Cholesky" | custom-call | tf_op jit(solution)/shard_map/jit(cholesky)/cholesky | solution.py:23
  213.1 0.7 compare_reduce_fusion
  215.3 4.3 %while.1 = (s32[]{:T(128)}, f32[256,256]{1,0:T(8,128)S(1)}, s32[2,2]{1,0:T(2,128)S(1)}, f32[2,128,128]{2,1,0:T(8,128)S(1)}, s32[]{:T(128)}) while((s32[]{:T(128)}, f32[256,256]{1,0:T(8,128)S(1)}, s32[2,2]{1,0:T(2,128)S(1)}, f32[2,128,128]{2,1,0:T(8,128)S(1)}, s32[]{:T(128)}) %tuple.28), condition=%wide.while_cond, body=%wide.while_body.sunk | while | flops 2 | bytes 131181 | solution.py:24
  216.1 1.4 bitcast_dynamic-update-slice_fusion.2
  218.1 1.4 bitcast_dynamic-update-slice_fusion.2
  220.2 20.5 %custom-call.16 = f32[2,128,128]{1,2,0:T(8,128)S(1)} custom-call(f32[2,128,128]{2,1,0:T(8,128)} %copy-done.4), custom_call_target="InvertDiagBlocksLowerTriangular" | custom-call | tf_op jit(solution)/shard_map/jit(_solve_triangular)/triangular_solve | solution.py:24
  241.4 1.0 convolution_subtract_fusion
  243.0 2.2 fusion.2
  245.3 1.0 maximum_bitcast_fusion
  246.3 2.5 copy.8
  248.8 34.3 %reduce-scatter.2.cloned.1.call-done = f32[32,1536]{1,0:T(8,128)} async-done(((f32[256,1536]{1,0:T(8,128)}), f32[32,1536]{1,0:T(8,128)}) %reduce-scatter.2.cloned.1.call-update) | async-done | bytes 196624 | tf_op jit(solution)/shard_map/reduce_scatter | solution.py:26
  283.1 1.6 broadcast_divide_fusion.1
  (36 shorter events, 5.6 us)
Async XLA Ops:
  7.2 2.1 copy-start
  7.2 112.3 %all-gather.3.cloned.1.call-start = ((), (), s32[]{:S(2)}) async-start(), calls=%async_computation.3 | async-start | bytes 5242880 | tf_op jit(solution)/shard_map/all_gather | solution.py:19
  9.2 24.7 %copy-start.3 = (bf16[1536,256]{1,0:T(8,128)(2,1)S(1)}, bf16[1536,256]{1,0:T(8,128)(2,1)}, u32[]{:S(2)}) copy-start(bf16[1536,256]{1,0:T(8,128)(2,1)} %param.6) | copy-start | bytes 2359300
  32.2 1.7 copy-start.1
  35.9 141.3 %all-reduce.3.cloned.1.call-start = ((), (), s32[]{:S(2)}) async-start(), calls=%async_computation.1 | async-start | bytes 524288 | tf_op jit(solution)/shard_map/psum | solution.py:22
  119.5 5.4 %copy-start.5 = (s32[8]{0:T(128)S(1)}, s32[8]{0:T(128)}, u32[]{:S(2)}) copy-start(s32[8]{0:T(128)} %param.7) | copy-start | bytes 100
  124.7 158.5 %reduce-scatter.2.cloned.1.call-start = ((), (), s32[]{:S(2)}) async-start(), calls=%async_computation.2 | async-start | bytes 1769472 | tf_op jit(solution)/shard_map/reduce_scatter | solution.py:26
  219.6 0.7 copy-start.4
  240.7 2.3 copy-start.2
Sparse Core Ops, SparseCore 0:
  36.0 83.4 all-gather.2
  124.8 52.3 all-reduce.2
  245.4 37.7 reduce-scatter.1
